TPU v7x, 256 devices: a whole 4x4x8 slice. The times are simulated.
256 devices in a mesh: row: 16 (over x, y), col: 16 (over z, core).
Axes of the slice: x: 4, y: 4, z: 8, core: 2. Of those that a mesh axis runs over, the one named last changes fastest.
Arguments:
- wrapped: float32 [1, 16384, 16384], P(None, 'row', 'col'), may hold values from -2.8 to 2.8
- col_steps: int32 [1, 16, 16], P(None, 'row', 'col'), may hold values from -2 to 2, as said below
- row_steps: int32 [1, 16, 16], P(None, 'row', 'col'), may hold values from -2 to 2, as said below
Outputs:
- unwrapped: float32 [1, 16384, 16384], P(None, 'row', 'col')
Inputs may be any that keep to these rules, and one draw needn't show every extreme that they name: `col_steps`: nonzero whole numbers; the last tile column has no edge. `row_steps`: nonzero whole numbers; the last tile row has no edge.
All inputs are finite; a program needn't handle non-finite values.
Results may differ from a plain program's by a relative error of at most 0.0003.
Values sent between devices are 32-bit elements; how exact they have to be, the bound alone decides.
A program may use at most 64 MiB of HBM per device.

v0:
```python
import math
import jax
import jax.numpy as jnp
from jax import lax
from jax.sharding import PartitionSpec as P

ITERS = 2
TWO_PI = 2.0 * math.pi


def with_halo(x, sides, width):
    edges = {}
    for axis, dim in sides:
        peers, length = (lax.axis_size(axis), x.shape[dim])
        up = [(i, (i + 1) % peers) for i in range(peers - 1)]
        last = lax.slice_in_dim(x, length - width, length, axis=dim)
        leading = lax.slice_in_dim(x, 0, width, axis=dim)
        edges[dim] = (
            lax.ppermute(last, axis, up),
            lax.ppermute(leading, axis, [(b, a) for a, b in up]),
        )
    done = []
    for _, dim in sides:
        low, high = edges[dim]
        around = [(width, width) if d in done else (0, 0) for d in range(x.ndim)]
        x = jnp.concatenate([jnp.pad(low, around), x, jnp.pad(high, around)], axis=dim)
        done.append(dim)
    return x


def gather_turned(arrays, axis, dims):
    turned = [jnp.moveaxis(a, dim, 0) for a, dim in zip(arrays, dims)]
    both = jnp.concatenate([t.reshape(len(t), -1) for t in turned], axis=1)
    result, at, finished = (lax.all_gather(both, axis, axis=0, tiled=True), 0, [])
    for t, dim in zip(turned, dims):
        piece = result[:, at : at + t[0].size].reshape(-1, *t.shape[1:])
        finished.append(jnp.moveaxis(piece, 0, dim))
        at += t[0].size
    return tuple(finished)


def wrap_diff(change):
    return change - TWO_PI * jnp.floor(change / TWO_PI + 0.5)


def running_sum(values):
    frames, tile_rows, tile_width = values.shape
    block_len = math.gcd(tile_width, 128)
    blocks_in = tile_width // block_len
    pieces = values.reshape(frames, tile_rows, blocks_in, block_len)
    strict_upper = (
        lax.broadcasted_iota(jnp.int32, (block_len, block_len), 0)
        < lax.broadcasted_iota(jnp.int32, (block_len, block_len), 1)
    ).astype(jnp.float32)
    inside = jnp.einsum("frcm,mk->frck", pieces, strict_upper, precision=lax.Precision.HIGHEST)
    totals = jnp.sum(pieces, axis=3)
    before = jnp.cumsum(totals, axis=2) - totals
    return (inside + before[:, :, :, None]).reshape(frames, tile_rows, tile_width)


def integrate_line(line):
    steps = wrap_diff(line[:, 1:] - line[:, :-1])
    running = jnp.cumsum(steps, axis=1)
    return line[:, 0:1] + jnp.concatenate([jnp.zeros_like(line[:, 0:1]), running], axis=1)


def mean_jump(own_edge, crossing, beyond, weights):
    return jnp.sum(weights * (own_edge + crossing - beyond), axis=1) / jnp.sum(weights, axis=1)


def on_device(wrapped, col_steps, row_steps):
    frames, tile_rows, tile_cols = wrapped.shape
    padded = with_halo(wrapped, (("row", 1), ("col", 2)), 1)
    step_x = wrap_diff(padded[:, :, 1:] - padded[:, :, :-1])
    step_y = wrap_diff(padded[:, 1:, :] - padded[:, :-1, :])
    charge_across = (
        step_x[:, 0:tile_rows, tile_cols - 1]
        + step_y[:, 0:tile_rows, tile_cols]
        - step_x[:, 1 : tile_rows + 1, tile_cols - 1]
        - step_y[:, 0:tile_rows, tile_cols - 1]
    ) / TWO_PI
    at_top = (lax.broadcasted_iota(jnp.int32, (1, tile_rows), 1) == 0) & (
        lax.axis_index("row") == 0
    )
    charge_across = jnp.where(at_top, 0.0, charge_across)
    charge_down = (
        step_x[:, tile_rows - 1, 0:tile_cols]
        + step_y[:, tile_rows - 1, 1 : tile_cols + 1]
        - step_x[:, tile_rows, 0:tile_cols]
        - step_y[:, tile_rows - 1, 0:tile_cols]
    ) / TWO_PI
    at_left = (lax.broadcasted_iota(jnp.int32, (1, tile_cols), 1) == 0) & (
        lax.axis_index("col") == 0
    )
    charge_down = jnp.where(at_left, 0.0, charge_down)
    weight_across = 1.0 / (1.0 + jnp.abs(charge_across))
    weight_down = 1.0 / (1.0 + jnp.abs(charge_down))
    crossing_x = step_x[:, 1 : tile_rows + 1, tile_cols]
    crossing_y = step_y[:, tile_rows, 1 : tile_cols + 1]
    column_steps = step_y[:, 1 : tile_rows + 1, 1]
    downward = jnp.cumsum(column_steps, axis=1) - column_steps
    anchor = wrapped[:, 0, 0]
    integrated = (anchor[:, None] + downward)[:, :, None] + running_sum(
        step_x[:, 1 : tile_rows + 1, 1 : tile_cols + 1]
    )
    cycles_across = TWO_PI * col_steps[:, 0, 0].astype(jnp.float32)
    cycles_down = TWO_PI * row_steps[:, 0, 0].astype(jnp.float32)
    right_first = integrate_line(padded[:, 1 : tile_rows + 1, tile_cols + 1])
    below_first = integrate_line(padded[:, tile_rows + 1, 1 : tile_cols + 1])
    base_across = (
        mean_jump(integrated[:, :, -1], crossing_x, right_first, weight_across) + cycles_across
    )
    base_down = mean_jump(integrated[:, -1, :], crossing_y, below_first, weight_down) + cycles_down
    grid_rows = lax.axis_size("row")
    grid_cols = lax.axis_size("col")
    every_across, every_down = gather_turned(
        (base_across[:, None], base_down[:, None]), ("row", "col"), (1, 1)
    )
    every_across = every_across.reshape(frames, grid_rows, grid_cols)
    every_down = every_down.reshape(frames, grid_rows, grid_cols)
    totals = jnp.zeros((frames, grid_rows, grid_cols), jnp.float32)
    for sweep in range(ITERS):
        right_total = jnp.concatenate(
            [totals[:, :, 1:], jnp.zeros((frames, grid_rows, 1), jnp.float32)], axis=2
        )
        below_total = jnp.concatenate(
            [totals[:, 1:, :], jnp.zeros((frames, 1, grid_cols), jnp.float32)], axis=1
        )
        horizontal = every_across + totals - right_total
        vertical = every_down + totals - below_total
        prefix_across = jnp.cumsum(horizontal, axis=2) - horizontal
        prefix_down = jnp.cumsum(vertical, axis=1) - vertical
        totals = totals + 0.5 * (
            prefix_across + prefix_across[:, 0:1, :] + prefix_down + prefix_down[:, :, 0:1]
        )
    mine = lax.dynamic_slice(
        totals, (0, lax.axis_index("row"), lax.axis_index("col")), (frames, 1, 1)
    )
    return (integrated + mine) / TWO_PI


def solution(mesh):
    in_specs = (P(None, "row", "col"), P(None, "row", "col"), P(None, "row", "col"))
    out_specs = P(None, "row", "col")
    return jax.shard_map(
        on_device, mesh=mesh, in_specs=in_specs, out_specs=out_specs, check_vma=False
    )
```

profile of v0, /device:TPU:1, one launch (start us, length us, event | category | flops | bytes accessed | tf_op | source)
XLA Modules:
  0.0 165.0 jit_solution(7441537384304579443)
XLA Ops:
  0.0 0.8 fusion.18
  0.8 0.2 copy.21
  1.0 4.1 %collective-permute-start.1 = (f32[1,1,1024]{1,2,0:T(8,128)S(1)}, f32[1,1,1024]{1,2,0:T(8,128)S(1)}, u32[]{:S(2)}, u32[]{:S(2)}) collective-permute-start(f32[1,1,1024]{1,2,0:T(8,128)S(1)} %copy.21), channel_id=1, source_target_pairs={{0,16},{16,32},{32,48},{48,64},{64,80},{80,96},{96,112},{112,128},... | collective-permute-start | bytes 12296 | tf_op jit(solution)/shard_map/ppermute | solution.py:19
  5.1 0.2 copy.22
  5.3 1.3 collective-permute-start.2
  6.6 5.3 %copy.20 = f32[1,1024,1024]{1,2,0:T(8,128)} copy(f32[1,1024,1024]{2,1,0:T(8,128)} %param.3) | data formatting | bytes 8388608 | tf_op args[0]
  11.9 0.8 fusion.17
  12.7 2.9 %collective-permute-start.3 = (f32[1,1024,1]{1,2,0:T(1,128)S(1)}, f32[1,1024,1]{1,2,0:T(1,128)S(1)}, u32[]{:S(2)}, u32[]{:S(2)}) collective-permute-start(f32[1,1024,1]{1,2,0:T(1,128)S(1)} %get-tuple-element.13), channel_id=1, source_target_pairs={{1,0},{2,1},{3,2},{4,3},{5,4},{6,5},{7,6},{8,7},{9,8},{10,9},{11,1... | collective-permute-start | bytes 12296 | tf_op jit(solution)/shard_map/ppermute | solution.py:20
  15.6 3.4 %collective-permute-start = (f32[1,1024,1]{1,2,0:T(1,128)S(1)}, f32[1,1024,1]{1,2,0:T(1,128)S(1)}, u32[]{:S(2)}, u32[]{:S(2)}) collective-permute-start(f32[1,1024,1]{1,2,0:T(1,128)S(1)} %get-tuple-element.14), channel_id=1, source_target_pairs={{0,1},{1,2},{2,3},{3,4},{4,5},{5,6},{6,7},{7,8},{8,9},{9,10},{10,1... | collective-permute-start | bytes 12296 | tf_op jit(solution)/shard_map/ppermute | solution.py:19
  19.1 1.3 slice.130
  21.6 0.2 reduce.10
  21.8 0.1 multiply_subtract_fusion.2
  22.0 0.6 slice.192
  22.6 0.5 slice.183
  23.2 6.4 %concatenate.59 = f32[1,1026,1024]{1,2,0:T(8,128)} concatenate(f32[1,1,1024]{1,2,0:T(8,128)S(1)} %collective-permute-done.1, f32[1,1024,1024]{1,2,0:T(8,128)} %copy.20, f32[1,1,1024]{1,2,0:T(8,128)S(1)} %collective-permute-done.2), dimensions={1} | concatenate | bytes 8404992 | tf_op jit(solution)/shard_map/concatenate | solution.py:26
  29.7 7.4 %multiply_subtract_fusion = f32[1,1026,1025]{1,2,0:T(8,128)} fusion(f32[1,1026,1024]{1,2,0:T(8,128)} %concatenate.59, f32[1,1026,1]{1,2,0:T(1,128)S(1)} %pad.15, f32[1,1026,1]{1,2,0:T(1,128)S(1)} %pad.16), kind=kLoop, calls=%fused_computation.2 | loop fusion | flops 8413200 | bytes 8417304 | tf_op jit(solution)/shard_map/sub | solution.py:43
  37.0 15.3 %concatenate.60 = f32[1,1026,1026]{1,2,0:T(8,128)} concatenate(f32[1,1026,1]{1,2,0:T(1,128)S(1)} %pad.15, f32[1,1026,1024]{1,2,0:T(8,128)} %concatenate.59, f32[1,1026,1]{1,2,0:T(1,128)S(1)} %pad.16), dimensions={2} | concatenate | bytes 8421408 | tf_op jit(solution)/shard_map/concatenate | solution.py:26
  52.3 0.3 reduce-window.26
  52.6 0.2 slice_reduce_fusion.4
  52.8 0.2 reduce-window.29
  53.0 0.3 reduce-window.24
  53.3 0.2 slice_reduce_fusion.5
  53.5 0.2 reduce-window.25
  53.6 5.1 %multiply_subtract_fusion.1 = f32[1,1025,1026]{1,2,0:T(8,128)S(1)} fusion(f32[1,1026,1026]{1,2,0:T(8,128)} %concatenate.60), kind=kLoop, calls=%fused_computation.3 | loop fusion | flops 6309900 | bytes 12619800 | tf_op jit(solution)/shard_map/sub | solution.py:43
  58.8 2.2 %copy-done.1 = f32[1,1025,1026]{1,2,0:T(8,128)} copy-done((f32[1,1025,1026]{1,2,0:T(8,128)}, f32[1,1025,1026]{1,2,0:T(8,128)S(1)}, u32[]{:S(2)}) %copy-start.1) | copy-done | bytes 4206624
  61.0 0.3 reduce-window.20
  61.3 0.2 slice_reduce_fusion.6
  61.5 0.2 reduce-window.21
  61.7 5.7 %slice.176 = f32[1,1024,1024]{1,2,0:T(8,128)} slice(f32[1,1026,1025]{1,2,0:T(8,128)} %multiply_subtract_fusion), slice={[0:1], [1:1025], [1:1025]} | slice | bytes 8388608 | tf_op jit(solution)/shard_map/slice | solution.py:104
  67.4 2.6 %reduce_sum.45 = f32[1024,8]{0,1:T(8,128)S(1)} reduce(f32[1024,8,128]{0,2,1:T(8,128)} %bitcast.62, f32[]{:T(128)} %constant.51.clone.1), dimensions={2}, to_apply=%region_2.3 | reduce | flops 1040384 | bytes 4227076 | tf_op jit(solution)/shard_map/reduce_sum | solution.py:56
  70.1 5.3 %convolution_add_fusion = f32[1024,8,128]{0,2,1:T(8,128)S(1)} fusion(f32[1024,8,128]{0,2,1:T(8,128)} %bitcast.63, f32[1024,8]{0,1:T(8,128)S(1)} %sub.200), kind=kOutput, calls=%fused_computation.6 | convolution fusion | flops 1611677696 | bytes 8421376 | tf_op jit(solution)/shard_map/frcm,mk->frck/dot_general | solution.py:55
  75.4 1.5 subtract_add_fusion
  77.0 0.8 bitcast_add_fusion
  77.8 2.6 %fusion = (f32[1024]{0:T(1024)S(1)}, f32[1024]{0:T(1024)S(1)}) fusion(f32[1,1025,1026]{1,2,0:T(8,128)} %copy-done.1, f32[1,1024,1024]{1,2,0:T(8,128)S(1)} %bitcast_add_fusion, f32[1,1026,1025]{1,2,0:T(8,128)} %multiply_subtract_fusion), kind=kLoop, calls=%fused_computation.8 | loop fusion | flops 5120 | bytes 32768 | tf_op jit(solution)/shard_map/add | solution.py:68
  80.6 2.9 %fusion.15 = (f32[]{:T(128)}, f32[]{:T(128)}, f32[]{:T(128)}, f32[]{:T(128)}) fusion(f32[1,1023]{1,0:T(1,128)S(1)} %slice_add_fusion.3, f32[1,1]{1,0:T(1,128)} %constant.59.clone.1, f32[]{:T(128)} %bitcast.12, f32[1,1026,1025]{1,2,0:T(8,128)} %multiply_subtract_fusion, f32[1,1024,1024]{1,2,0:T(8,128)S(1)} %bitcast_add_fusion, f32[1,1025,1026]{1,2,0:T(8,128)} %copy-done.1, ...), kind=kLoop, calls=%fused_computation.62 | loop fusion | flops 28668 | bytes 40982 | tf_op jit(solution)/shard_map/reduce_sum | solution.py:68
  86.2 60.9 %all-gather = f32[256,1,2]{2,1,0:T(1,128)S(1)} all-gather(f32[1,1,2]{2,1,0:T(1,128)S(1)} %maximum_bitcast_fusion), channel_id=1, replica_groups=mesh['row'=16,'col'=16] {'row','col'}, dimensions={0}, use_global_device_ids=true | all-gather | bytes 2056 | tf_op jit(solution)/shard_map/all_gather | solution.py:34
  147.2 0.2 slice_reduce_fusion.1
  147.6 0.1 slice_reduce_fusion.3
  147.7 0.2 reduce_window_sum.106
  148.1 0.1 slice_reduce_fusion.2
  148.2 0.2 reduce_window_sum.108
  148.4 0.7 dynamic-slice.1
  149.1 0.6 dynamic-slice
  149.6 1.2 fusion.19
  150.8 1.2 fusion.20
  153.4 0.6 fusion.21
  154.0 5.7 %add_multiply_fusion = f32[1,1024,1024]{1,2,0:T(8,128)} fusion(f32[]{:T(128)} %bitcast.32, f32[1024,8,128]{0,2,1:T(8,128)} %copy-done, f32[1024]{0:T(1024)S(1)} %bitcast.66), kind=kLoop, calls=%fused_computation.5 | loop fusion | flops 3145728 | bytes 8392708 | tf_op jit(solution)/shard_map/div | solution.py:139
  159.7 5.3 %copy.26 = f32[1,1024,1024]{2,1,0:T(8,128)} copy(f32[1,1024,1024]{1,2,0:T(8,128)} %add_multiply_fusion) | data formatting | bytes 8388608 | tf_op jit(solution)/shard_map/div | solution.py:139
  (38 shorter events, 1.1 us)
Async XLA Ops:
  1.0 22.1 %collective-permute-start.1 = (f32[1,1,1024]{1,2,0:T(8,128)S(1)}, f32[1,1,1024]{1,2,0:T(8,128)S(1)}, u32[]{:S(2)}, u32[]{:S(2)}) collective-permute-start(f32[1,1,1024]{1,2,0:T(8,128)S(1)} %copy.21), channel_id=1, source_target_pairs={{0,16},{16,32},{32,48},{48,64},{64,80},{80,96},{96,112},{112,128},... | collective-permute-start | bytes 12296 | tf_op jit(solution)/shard_map/ppermute | solution.py:19
  5.3 16.3 %collective-permute-start.2 = (f32[1,1,1024]{1,2,0:T(8,128)S(1)}, f32[1,1,1024]{1,2,0:T(8,128)S(1)}, u32[]{:S(2)}, u32[]{:S(2)}) collective-permute-start(f32[1,1,1024]{1,2,0:T(8,128)S(1)} %copy.22), channel_id=1, source_target_pairs={{16,0},{32,16},{48,32},{64,48},{80,64},{96,80},{112,96},{128,112},... | collective-permute-start | bytes 12296 | tf_op jit(solution)/shard_map/ppermute | solution.py:20
  12.7 9.2 %collective-permute-start.3 = (f32[1,1024,1]{1,2,0:T(1,128)S(1)}, f32[1,1024,1]{1,2,0:T(1,128)S(1)}, u32[]{:S(2)}, u32[]{:S(2)}) collective-permute-start(f32[1,1024,1]{1,2,0:T(1,128)S(1)} %get-tuple-element.13), channel_id=1, source_target_pairs={{1,0},{2,1},{3,2},{4,3},{5,4},{6,5},{7,6},{8,7},{9,8},{10,9},{11,1... | collective-permute-start | bytes 12296 | tf_op jit(solution)/shard_map/ppermute | solution.py:20
  15.6 14.0 %collective-permute-start = (f32[1,1024,1]{1,2,0:T(1,128)S(1)}, f32[1,1024,1]{1,2,0:T(1,128)S(1)}, u32[]{:S(2)}, u32[]{:S(2)}) collective-permute-start(f32[1,1024,1]{1,2,0:T(1,128)S(1)} %get-tuple-element.14), channel_id=1, source_target_pairs={{0,1},{1,2},{2,3},{3,4},{4,5},{5,6},{6,7},{7,8},{8,9},{9,10},{10,1... | collective-permute-start | bytes 12296 | tf_op jit(solution)/shard_map/ppermute | solution.py:19
  58.7 2.2 %copy-start.1 = (f32[1,1025,1026]{1,2,0:T(8,128)}, f32[1,1025,1026]{1,2,0:T(8,128)S(1)}, u32[]{:S(2)}) copy-start(f32[1,1025,1026]{1,2,0:T(8,128)S(1)} %multiply_subtract_fusion.1) | copy-start | bytes 12619804
  75.4 5.1 %copy-start = (f32[1024,8,128]{0,2,1:T(8,128)}, f32[1024,8,128]{0,2,1:T(8,128)S(1)}, u32[]{:S(2)}) copy-start(f32[1024,8,128]{0,2,1:T(8,128)S(1)} %convolution_add_fusion) | copy-start | bytes 12582916
where the time goes:
time: 166 us; the launch traced here: 165 us
  blocking collectives  60.9 us (37%)
  local copies, waits for them, and re-layouts  47.6 us (29%)
  other arithmetic  34.1 us (21%)
  starting transfers between devices  11.6 us (7%)
  between operations  5.5 us (3%)
  matrix products  5.29 us (3%)
    all_gather x1, blocking collectives, gather_turned(): lax.all_gather(both, axis, axis=0, tiled=True)  60.9 us
    concatenate x2, local copies, waits for them, and re-layouts, with_halo(): jnp.concatenate([jnp.pad(low, around), x, jnp.pad(high, around)], axis=dim)  21.6 us
    sub x4, other arithmetic, wrap_diff(): return change - TWO_PI * jnp.floor(change / TWO_PI + 0.5)  12.6 us
    unnamed x5, local copies, waits for them, and re-layouts  7.52 us
    ppermute x2, starting transfers between devices, with_halo(): lax.ppermute(last, axis, up)  7.49 us
    slice x1, local copies, waits for them, and re-layouts, on_device(): step_x[:, 1:tile_rows + 1, 1:tile_cols + 1]  5.75 us
    div x1, other arithmetic, on_device(): return (integrated + mine) / TWO_PI  5.7 us
    div x1, local copies, waits for them, and re-layouts, on_device(): return (integrated + mine) / TWO_PI  5.34 us
  transfers between devices with their start and end apart: 4, of which 0 were waited for; matrix products, arithmetic and copies ran while one was open for 9% of the time, Pallas kernels for 0%

commit v1 on v0

--- a/solution.py
+++ b/solution.py
@@ -31,7 +31,13 @@
 def gather_turned(arrays, axis, dims):
     turned = [jnp.moveaxis(a, dim, 0) for a, dim in zip(arrays, dims)]
     both = jnp.concatenate([t.reshape(len(t), -1) for t in turned], axis=1)
-    result, at, finished = (lax.all_gather(both, axis, axis=0, tiled=True), 0, [])
+    result, at, finished = (
+        jnp.concatenate(
+            lax.all_to_all(jnp.stack([both] * lax.axis_size(axis)), axis, 0, 0), axis=0
+        ),
+        0,
+        [],
+    )
     for t, dim in zip(turned, dims):
         piece = result[:, at : at + t[0].size].reshape(-1, *t.shape[1:])
         finished.append(jnp.moveaxis(piece, 0, dim))

time: 166 us -> 134 us (0.81)
  blocking collectives: 60.9 us -> 0 us
  starting transfers between devices: 11.6 us -> 26.9 us
  waiting for transfers between devices: 0.01 us -> 12.9 us
    all_gather x1 -> x0, blocking collectives: 60.9 us -> none  [gather_turned(): lax.all_gather(both, axis, axis=0, tiled=True)]
    all_to_all x0 -> x1, starting transfers between devices: none -> 15.2 us  [gather_turned(): lax.all_to_all(jnp.stack([both] * lax.axis_size(axis)), axis, 0, 0)]
    all_to_all x0 -> x1, waiting for transfers between devices: none -> 12.9 us  [gather_turned(): lax.all_to_all(jnp.stack([both] * lax.axis_size(axis)), axis, 0, 0)]
  transfers between devices with their start and end apart: 4 -> 5, of which waited for: 0 -> 1; matrix products, arithmetic and copies ran while one was open for 9% -> 12% of each run, Pallas kernels for 0% -> 0%
where the time goes in v1:
time: 134 us; the launch traced here: 133 us
  local copies, waits for them, and re-layouts  48.3 us (36%)
  other arithmetic  34.1 us (25%)
  starting transfers between devices  26.9 us (20%)
  waiting for transfers between devices  12.9 us (10%)
  between operations  5.5 us (4%)
  matrix products  5.29 us (4%)
    concatenate x2, local copies, waits for them, and re-layouts, with_halo(): jnp.concatenate([jnp.pad(low, around), x, jnp.pad(high, around)], axis=dim)  21.6 us
    all_to_all x1, starting transfers between devices, gather_turned(): lax.all_to_all(jnp.stack([both] * lax.axis_size(axis)), axis, 0, 0)  15.2 us
    all_to_all x1, waiting for transfers between devices, gather_turned(): lax.all_to_all(jnp.stack([both] * lax.axis_size(axis)), axis, 0, 0)  12.9 us
    sub x4, other arithmetic, wrap_diff(): return change - TWO_PI * jnp.floor(change / TWO_PI + 0.5)  12.6 us
    unnamed x5, local copies, waits for them, and re-layouts  7.52 us
    ppermute x2, starting transfers between devices, with_halo(): lax.ppermute(last, axis, up)  7.49 us
    slice x1, local copies, waits for them, and re-layouts, on_device(): step_x[:, 1:tile_rows + 1, 1:tile_cols + 1]  5.75 us
    div x1, other arithmetic, on_device(): return (integrated + mine) / TWO_PI  5.7 us
  transfers between devices with their start and end apart: 5, of which 1 were waited for; matrix products, arithmetic and copies ran while one was open for 12% of the time, Pallas kernels for 0%

profile of v1, /device:TPU:1, one launch (start us, length us, event | category | flops | bytes accessed | tf_op | source)
XLA Modules:
  0.0 133.0 jit_solution(1934995955906061356)
XLA Ops:
  0.0 0.8 fusion.18
  0.8 0.2 copy.28
  1.0 4.1 %collective-permute-start.1 = (f32[1,1,1024]{1,2,0:T(8,128)S(1)}, f32[1,1,1024]{1,2,0:T(8,128)S(1)}, u32[]{:S(2)}, u32[]{:S(2)}) collective-permute-start(f32[1,1,1024]{1,2,0:T(8,128)S(1)} %copy.28), channel_id=1, source_target_pairs={{0,16},{16,32},{32,48},{48,64},{64,80},{80,96},{96,112},{112,128},... | collective-permute-start | bytes 12296 | tf_op jit(solution)/shard_map/ppermute | solution.py:19
  5.1 0.2 copy.29
  5.3 1.3 collective-permute-start.2
  6.6 5.3 %copy.27 = f32[1,1024,1024]{1,2,0:T(8,128)} copy(f32[1,1024,1024]{2,1,0:T(8,128)} %param.3) | data formatting | bytes 8388608 | tf_op args[0]
  11.9 0.8 fusion.17
  12.7 2.9 %collective-permute-start.3 = (f32[1,1024,1]{1,2,0:T(1,128)S(1)}, f32[1,1024,1]{1,2,0:T(1,128)S(1)}, u32[]{:S(2)}, u32[]{:S(2)}) collective-permute-start(f32[1,1024,1]{1,2,0:T(1,128)S(1)} %get-tuple-element.13), channel_id=1, source_target_pairs={{1,0},{2,1},{3,2},{4,3},{5,4},{6,5},{7,6},{8,7},{9,8},{10,9},{11,1... | collective-permute-start | bytes 12296 | tf_op jit(solution)/shard_map/ppermute | solution.py:20
  15.6 3.4 %collective-permute-start = (f32[1,1024,1]{1,2,0:T(1,128)S(1)}, f32[1,1024,1]{1,2,0:T(1,128)S(1)}, u32[]{:S(2)}, u32[]{:S(2)}) collective-permute-start(f32[1,1024,1]{1,2,0:T(1,128)S(1)} %get-tuple-element.14), channel_id=1, source_target_pairs={{0,1},{1,2},{2,3},{3,4},{4,5},{5,6},{6,7},{7,8},{8,9},{9,10},{10,1... | collective-permute-start | bytes 12296 | tf_op jit(solution)/shard_map/ppermute | solution.py:19
  19.0 1.3 slice.130
  21.6 0.2 reduce.10
  22.0 0.6 slice.192
  22.6 0.5 slice.183
  23.1 6.4 %concatenate.61 = f32[1,1026,1024]{1,2,0:T(8,128)} concatenate(f32[1,1,1024]{1,2,0:T(8,128)S(1)} %collective-permute-done.1, f32[1,1024,1024]{1,2,0:T(8,128)} %copy.27, f32[1,1,1024]{1,2,0:T(8,128)S(1)} %collective-permute-done.2), dimensions={1} | concatenate | bytes 8404992 | tf_op jit(solution)/shard_map/concatenate | solution.py:26
  29.7 7.4 %multiply_subtract_fusion = f32[1,1026,1025]{1,2,0:T(8,128)} fusion(f32[1,1026,1024]{1,2,0:T(8,128)} %concatenate.61, f32[1,1026,1]{1,2,0:T(1,128)S(1)} %pad.15, f32[1,1026,1]{1,2,0:T(1,128)S(1)} %pad.16), kind=kLoop, calls=%fused_computation.2 | loop fusion | flops 8413200 | bytes 8417304 | tf_op jit(solution)/shard_map/sub | solution.py:49
  37.0 15.3 %concatenate.62 = f32[1,1026,1026]{1,2,0:T(8,128)} concatenate(f32[1,1026,1]{1,2,0:T(1,128)S(1)} %pad.15, f32[1,1026,1024]{1,2,0:T(8,128)} %concatenate.61, f32[1,1026,1]{1,2,0:T(1,128)S(1)} %pad.16), dimensions={2} | concatenate | bytes 8421408 | tf_op jit(solution)/shard_map/concatenate | solution.py:26
  52.3 0.3 reduce-window.26
  52.6 0.2 slice_reduce_fusion.4
  52.8 0.2 reduce-window.29
  53.0 0.3 reduce-window.24
  53.3 0.2 slice_reduce_fusion.5
  53.4 0.2 reduce-window.25
  53.6 5.1 %multiply_subtract_fusion.1 = f32[1,1025,1026]{1,2,0:T(8,128)S(1)} fusion(f32[1,1026,1026]{1,2,0:T(8,128)} %concatenate.62), kind=kLoop, calls=%fused_computation.3 | loop fusion | flops 6309900 | bytes 12619800 | tf_op jit(solution)/shard_map/sub | solution.py:49
  58.7 2.2 %copy-done.1 = f32[1,1025,1026]{1,2,0:T(8,128)} copy-done((f32[1,1025,1026]{1,2,0:T(8,128)}, f32[1,1025,1026]{1,2,0:T(8,128)S(1)}, u32[]{:S(2)}) %copy-start.1) | copy-done | bytes 4206624
  61.0 0.3 reduce-window.20
  61.3 0.2 slice_reduce_fusion.6
  61.5 0.2 reduce-window.21
  61.6 5.7 %slice.176 = f32[1,1024,1024]{1,2,0:T(8,128)} slice(f32[1,1026,1025]{1,2,0:T(8,128)} %multiply_subtract_fusion), slice={[0:1], [1:1025], [1:1025]} | slice | bytes 8388608 | tf_op jit(solution)/shard_map/slice | solution.py:110
  67.4 2.6 %reduce_sum.45 = f32[1024,8]{0,1:T(8,128)S(1)} reduce(f32[1024,8,128]{0,2,1:T(8,128)} %bitcast.62, f32[]{:T(128)} %constant.51.clone.1), dimensions={2}, to_apply=%region_2.3 | reduce | flops 1040384 | bytes 4227076 | tf_op jit(solution)/shard_map/reduce_sum | solution.py:62
  70.1 5.3 %convolution_add_fusion = f32[1024,8,128]{0,2,1:T(8,128)S(1)} fusion(f32[1024,8,128]{0,2,1:T(8,128)} %bitcast.63, f32[1024,8]{0,1:T(8,128)S(1)} %sub.200), kind=kOutput, calls=%fused_computation.6 | convolution fusion | flops 1611677696 | bytes 8421376 | tf_op jit(solution)/shard_map/frcm,mk->frck/dot_general | solution.py:61
  75.4 1.5 %subtract_add_fusion = f32[1,1024,1]{1,2,0:T(1,128)S(1)} fusion(f32[1,1024,1]{1,2,0:T(1,128)S(1)} %bitcast.73, f32[1,1024,1]{1,2,0:T(1,128)S(1)} %bitcast.81, f32[]{:T(128)} %bitcast, f32[1,1025,1026]{1,2,0:T(8,128)} %copy-done.1), kind=kLoop, calls=%fused_computation.49 | loop fusion | flops 3072 | bytes 16388 | tf_op jit(solution)/shard_map/add | solution.py:109
  77.0 0.8 bitcast_add_fusion
  77.8 2.6 %fusion = (f32[1024]{0:T(1024)S(1)}, f32[1024]{0:T(1024)S(1)}) fusion(f32[1,1025,1026]{1,2,0:T(8,128)} %copy-done.1, f32[1,1024,1024]{1,2,0:T(8,128)S(1)} %bitcast_add_fusion, f32[1,1026,1025]{1,2,0:T(8,128)} %multiply_subtract_fusion), kind=kLoop, calls=%fused_computation.8 | loop fusion | flops 5120 | bytes 32768 | tf_op jit(solution)/shard_map/add | solution.py:74
  80.6 2.9 %fusion.15 = (f32[]{:T(128)}, f32[]{:T(128)}, f32[]{:T(128)}, f32[]{:T(128)}) fusion(f32[1,1023]{1,0:T(1,128)S(1)} %slice_add_fusion.3, f32[1,1]{1,0:T(1,128)} %constant.59.clone.1, f32[]{:T(128)} %bitcast.12, f32[1,1026,1025]{1,2,0:T(8,128)} %multiply_subtract_fusion, f32[1,1024,1024]{1,2,0:T(8,128)S(1)} %bitcast_add_fusion, f32[1,1025,1026]{1,2,0:T(8,128)} %copy-done.1, ...), kind=kLoop, calls=%fused_computation.62 | loop fusion | flops 28668 | bytes 40982 | tf_op jit(solution)/shard_map/reduce_sum | solution.py:74
  86.2 0.7 stack.2
  86.9 15.2 %all-to-all-start = ((f32[256,1,2]{2,1,0:T(1,128)}), f32[256,1,2]{2,1,0:T(1,128)S(1)}, u32[]{:S(2)}, u32[]{:S(2)}) async-start(f32[256,1,2]{2,1,0:T(1,128)} %stack.2), calls=%async_computation | async-start | bytes 262144 | tf_op jit(solution)/shard_map/all_to_all | solution.py:36
  102.2 12.9 %all-to-all-done = f32[256,1,2]{2,1,0:T(1,128)S(1)} async-done(((f32[256,1,2]{2,1,0:T(1,128)}), f32[256,1,2]{2,1,0:T(1,128)S(1)}, u32[]{:S(2)}, u32[]{:S(2)}) %all-to-all-start) | async-done | bytes 2080 | tf_op jit(solution)/shard_map/all_to_all | solution.py:36
  115.1 0.2 slice_reduce_fusion.1
  115.5 0.1 slice_reduce_fusion.3
  115.6 0.2 reduce_window_sum.106
  116.2 0.2 reduce_window_sum.108
  116.3 0.7 dynamic-slice.1
  117.0 0.6 dynamic-slice
  117.6 1.2 fusion.19
  118.8 1.2 fusion.20
  121.3 0.6 fusion.21
  121.9 5.7 %add_multiply_fusion = f32[1,1024,1024]{1,2,0:T(8,128)} fusion(f32[]{:T(128)} %bitcast.32, f32[1024,8,128]{0,2,1:T(8,128)} %copy-done, f32[1024]{0:T(1024)S(1)} %bitcast.66), kind=kLoop, calls=%fused_computation.5 | loop fusion | flops 3145728 | bytes 8392708 | tf_op jit(solution)/shard_map/div | solution.py:145
  127.6 5.3 %copy.33 = f32[1,1024,1024]{2,1,0:T(8,128)} copy(f32[1,1024,1024]{1,2,0:T(8,128)} %add_multiply_fusion) | data formatting | bytes 8388608 | tf_op jit(solution)/shard_map/div | solution.py:145
  (40 shorter events, 1.3 us)
Async XLA Ops:
  1.0 22.1 %collective-permute-start.1 = (f32[1,1,1024]{1,2,0:T(8,128)S(1)}, f32[1,1,1024]{1,2,0:T(8,128)S(1)}, u32[]{:S(2)}, u32[]{:S(2)}) collective-permute-start(f32[1,1,1024]{1,2,0:T(8,128)S(1)} %copy.28), channel_id=1, source_target_pairs={{0,16},{16,32},{32,48},{48,64},{64,80},{80,96},{96,112},{112,128},... | collective-permute-start | bytes 12296 | tf_op jit(solution)/shard_map/ppermute | solution.py:19
  5.3 16.3 %collective-permute-start.2 = (f32[1,1,1024]{1,2,0:T(8,128)S(1)}, f32[1,1,1024]{1,2,0:T(8,128)S(1)}, u32[]{:S(2)}, u32[]{:S(2)}) collective-permute-start(f32[1,1,1024]{1,2,0:T(8,128)S(1)} %copy.29), channel_id=1, source_target_pairs={{16,0},{32,16},{48,32},{64,48},{80,64},{96,80},{112,96},{128,112},... | collective-permute-start | bytes 12296 | tf_op jit(solution)/shard_map/ppermute | solution.py:20
  12.7 9.2 %collective-permute-start.3 = (f32[1,1024,1]{1,2,0:T(1,128)S(1)}, f32[1,1024,1]{1,2,0:T(1,128)S(1)}, u32[]{:S(2)}, u32[]{:S(2)}) collective-permute-start(f32[1,1024,1]{1,2,0:T(1,128)S(1)} %get-tuple-element.13), channel_id=1, source_target_pairs={{1,0},{2,1},{3,2},{4,3},{5,4},{6,5},{7,6},{8,7},{9,8},{10,9},{11,1... | collective-permute-start | bytes 12296 | tf_op jit(solution)/shard_map/ppermute | solution.py:20
  15.6 14.0 %collective-permute-start = (f32[1,1024,1]{1,2,0:T(1,128)S(1)}, f32[1,1024,1]{1,2,0:T(1,128)S(1)}, u32[]{:S(2)}, u32[]{:S(2)}) collective-permute-start(f32[1,1024,1]{1,2,0:T(1,128)S(1)} %get-tuple-element.14), channel_id=1, source_target_pairs={{0,1},{1,2},{2,3},{3,4},{4,5},{5,6},{6,7},{7,8},{8,9},{9,10},{10,1... | collective-permute-start | bytes 12296 | tf_op jit(solution)/shard_map/ppermute | solution.py:19
  58.7 2.2 %copy-start.1 = (f32[1,1025,1026]{1,2,0:T(8,128)}, f32[1,1025,1026]{1,2,0:T(8,128)S(1)}, u32[]{:S(2)}) copy-start(f32[1,1025,1026]{1,2,0:T(8,128)S(1)} %multiply_subtract_fusion.1) | copy-start | bytes 12619804
  75.4 5.1 %copy-start = (f32[1024,8,128]{0,2,1:T(8,128)}, f32[1024,8,128]{0,2,1:T(8,128)S(1)}, u32[]{:S(2)}) copy-start(f32[1024,8,128]{0,2,1:T(8,128)S(1)} %convolution_add_fusion) | copy-start | bytes 12582916
  86.9 28.2 %all-to-all-start = ((f32[256,1,2]{2,1,0:T(1,128)}), f32[256,1,2]{2,1,0:T(1,128)S(1)}, u32[]{:S(2)}, u32[]{:S(2)}) async-start(f32[256,1,2]{2,1,0:T(1,128)} %stack.2), calls=%async_computation | async-start | bytes 262144 | tf_op jit(solution)/shard_map/all_to_all | solution.py:36
